TPU v7x, 32 devices: a whole 2x2x4 slice. The times are simulated.
32 devices in a mesh: gx: 2 (over x), gy: 4 (over y, core), gz: 4 (over z).
Axes of the slice: x: 2, y: 2, z: 4, core: 2. Of those that a mesh axis runs over, the one named last changes fastest.
Arguments:
- estimate: float32 [48, 128, 512], P('gx', 'gy', 'gz'), may hold values from 0.03 to 11, as said below
- view_images: float32 [4, 48, 128, 512], P(None, 'gx', 'gy', 'gz'), may hold values from 0.015 to 21, as said below
- psf_taps: int32 [4, 3, 31], replicated, may hold values from 1 to 64
- view_weights: int32 [4], replicated, may hold values from 1 to 4
Outputs:
- deconvolved: float32 [48, 128, 512], P('gx', 'gy', 'gz')
- misfit: float32 [2, 4], replicated
Inputs may be any that keep to these rules, and one draw needn't show every extreme that they name: `estimate`: positive. `view_images`: positive.
All inputs are finite; a program needn't handle non-finite values.
Results may differ from a plain program's by a relative error of at most 0.0001.
Values sent between devices are 32-bit elements; how exact they have to be, the bound alone decides.
A program may use at most 128 MiB of HBM per device.

v0:
```python
import jax
import jax.numpy as jnp
from jax import lax
from jax.sharding import PartitionSpec as P

TAPS = 31
ITERS = 2


def extended(block, sides, width):
    for axis, dim in sides:
        count = lax.axis_size(axis)
        forward = [(i, i + 1) for i in range(count - 1)]
        backward = [(target, source) for source, target in forward]
        low = lax.ppermute(
            lax.slice_in_dim(block, block.shape[dim] - width, None, axis=dim), axis, forward
        )
        high = lax.ppermute(lax.slice_in_dim(block, 0, width, axis=dim), axis, backward)
        block = jnp.concatenate([low, block, high], axis=dim)
    return block


def toeplitz(kernels, length):
    span = kernels.shape[-1]
    offsets = jnp.arange(length + span - 1)[:, None] - jnp.arange(length)[None, :]
    indicator = (offsets[:, :, None] == jnp.arange(span)[None, None, :]).astype(jnp.float32)
    return jnp.einsum("vt,jit->vji", kernels, indicator, precision=lax.Precision.HIGHEST)


def product(form, left, right):
    return jnp.einsum(form, left, right, precision=lax.Precision.HIGHEST)


def local(estimate, view_images, psf_taps, view_weights):
    halo_width = (TAPS - 1) // 2
    cells_x, cells_y, cells_z = estimate.shape
    kernels = psf_taps.astype(jnp.float32) / 256.0
    flipped = kernels[:, :, ::-1]
    forward_x = toeplitz(kernels[:, 0], cells_x)
    forward_y = toeplitz(kernels[:, 1], cells_y)
    forward_z = toeplitz(kernels[:, 2], cells_z)
    backward_x = toeplitz(flipped[:, 0], cells_x)
    backward_y = toeplitz(flipped[:, 1], cells_y)
    backward_z = toeplitz(flipped[:, 2], cells_z)
    tap_sums = jnp.sum(kernels, axis=2)
    weight_float = view_weights.astype(jnp.float32)
    normalizer = jnp.sum(weight_float * jnp.prod(tap_sums, axis=1))
    backward_z = backward_z * (weight_float / normalizer)[:, None, None]
    data_total, data_square = lax.psum(
        (jnp.sum(view_images, axis=(1, 2, 3)), jnp.sum(view_images * view_images, axis=(1, 2, 3))),
        ("gx", "gy", "gz"),
    )
    misfits = []
    for iteration in range(ITERS):
        padded = extended(estimate, (("gx", 0),), halo_width)
        partial_value = product("jyz,vji->viyz", padded, forward_x)
        padded = extended(partial_value, (("gy", 2),), halo_width)
        partial_value = product("vxjz,vji->vxiz", padded, forward_y)
        padded = extended(partial_value, (("gz", 3),), halo_width)
        blurred = product("vxyj,vji->vxyi", padded, forward_z)
        local_total = jnp.sum(blurred, axis=(1, 2, 3))
        blurred_total, cross_total, blurred_square = lax.psum(
            (
                local_total,
                jnp.sum(view_images * blurred, axis=(1, 2, 3)),
                jnp.sum(blurred * blurred, axis=(1, 2, 3)),
            ),
            ("gx", "gy", "gz"),
        )
        flux_scale = data_total / blurred_total
        scaled = flux_scale[:, None, None, None] * blurred
        squared = (
            data_square - 2.0 * flux_scale * cross_total + flux_scale * flux_scale * blurred_square
        )
        misfits.append(squared / data_square)
        quotient = view_images / scaled
        padded = extended(quotient, (("gx", 1),), halo_width)
        partial_value = product("vjyz,vji->viyz", padded, backward_x)
        padded = extended(partial_value, (("gy", 2),), halo_width)
        partial_value = product("vxjz,vji->vxiz", padded, backward_y)
        padded = extended(partial_value, (("gz", 3),), halo_width)
        correction = product("vxyj,vji->xyi", padded, backward_z)
        estimate = estimate * correction
    return (estimate, jnp.stack(misfits))


def solution(mesh):
    placed = (P("gx", "gy", "gz"), P(None, "gx", "gy", "gz"), P(), P())
    return jax.shard_map(
        local, mesh=mesh, in_specs=placed, out_specs=(P("gx", "gy", "gz"), P()), check_vma=False
    )
```

profile of v0, /device:TPU:1, one launch (start us, length us, event | category | flops | bytes accessed | tf_op | source)
XLA Modules:
  0.0 385.9 jit_solution(9284746550260880942)
XLA Ops:
  1.9 3.9 %collective-permute-start = (f32[15,32,128]{2,0,1:T(8,128)S(1)}, f32[15,32,128]{2,0,1:T(8,128)S(1)}, u32[]{:S(2)}, u32[]{:S(2)}) collective-permute-start(f32[15,32,128]{2,0,1:T(8,128)S(1)} %get-tuple-element.42), channel_id=1, source_target_pairs={{0,16},{1,17},{2,18},{3,19},{4,20},{5,21},{6,22},{7,23},{8,24},{9,... | collective-permute-start | bytes 737288 | tf_op jit(solution)/shard_map/ppermute | solution.py:15
  7.5 3.3 collective-permute-done
  10.8 3.8 collective-permute-done.1
  16.2 4.8 %collective-permute-start.2 = (f32[4,24,15,128]{3,1,2,0:T(8,128)S(1)}, f32[4,24,15,128]{3,1,2,0:T(8,128)S(1)}, u32[]{:S(2)}, u32[]{:S(2)}) collective-permute-start(f32[4,24,15,128]{3,1,2,0:T(8,128)S(1)} %get-tuple-element.38), channel_id=1, source_target_pairs={{0,4},{4,8},{8,12},{1,5},{5,9},{9,13},{2,6},{6,10},{10,14},{3,7},{... | collective-permute-start | bytes 2211848 | tf_op jit(solution)/shard_map/ppermute | solution.py:15
  23.3 6.2 %collective-permute-done.2 = f32[4,24,15,128]{3,1,2,0:T(8,128)S(1)} collective-permute-done((f32[4,24,15,128]{3,1,2,0:T(8,128)S(1)}, f32[4,24,15,128]{3,1,2,0:T(8,128)S(1)}, u32[]{:S(2)}, u32[]{:S(2)}) %collective-permute-start.2) | collective-permute-done | bytes 737312 | tf_op jit(solution)/shard_map/ppermute | solution.py:15
  29.4 4.4 %collective-permute-done.3 = f32[4,24,15,128]{3,1,2,0:T(8,128)S(1)} collective-permute-done((f32[4,24,15,128]{3,1,2,0:T(8,128)S(1)}, f32[4,24,15,128]{3,1,2,0:T(8,128)S(1)}, u32[]{:S(2)}, u32[]{:S(2)}) %collective-permute-start.3) | collective-permute-done | bytes 737312 | tf_op jit(solution)/shard_map/ppermute | solution.py:18
  38.0 3.0 copy.36
  40.9 4.1 %collective-permute-start.4 = (f32[4,24,32,15]{2,1,3,0:T(8,128)}, f32[4,24,32,15]{2,1,3,0:T(8,128)}, u32[]{:S(2)}, u32[]{:S(2)}) collective-permute-start(f32[4,24,32,15]{2,1,3,0:T(8,128)} %copy.36), channel_id=1, source_target_pairs={{0,1},{1,2},{2,3},{4,5},{5,6},{6,7},{8,9},{9,10},{10,11},{12,13},{... | collective-permute-start | bytes 552968 | tf_op jit(solution)/shard_map/ppermute | solution.py:15
  49.3 3.5 collective-permute-done.4
  52.8 2.9 copy.38
  55.8 3.3 collective-permute-done.5
  62.0 7.1 %multiply_reduce_fusion.3 = (f32[4]{0:T(128)S(1)}, f32[4]{0:T(128)S(1)}, f32[4]{0:T(128)S(1)}, f32[4]{0:T(128)}, f32[4]{0:T(128)S(1)}, /*index=5*/f32[4,24,32,128]{3,2,1,0:T(8,128)}) fusion(f32[4,24,32,128]{3,2,1,0:T(8,128)S(1)} %copy-done, f32[4,158,128,1]{2,0,1,3:T(4,128)S(1)} %fusion.64, f32[4,24,32,15]{3,2,1,0:T(8,128)} %copy.39, ...), kind=kOutput, calls=%fused_computation.48 | convolution fusion | flops 749654016 | bytes 5410896 | tf_op jit(solution)/shard_map/vxyj,vji->vxyi/dot_general | solution.py:31
  69.1 36.8 %all-reduce.1 = (f32[4]{0:T(128)S(1)}, f32[4]{0:T(128)S(1)}) all-reduce(f32[4]{0:T(128)S(1)} %get-tuple-element.6, f32[4]{0:T(128)S(1)} %get-tuple-element.4), channel_id=1, replica_groups=mesh['gx'=2,'gy'=4,'gz'=4] {'gx','gy','gz'}, use_global_device_ids=true, to_apply=%region_1.0 | all-reduce | flops 8 | bytes 64 | tf_op jit(solution)/shard_map/psum | solution.py:49
  109.3 5.3 %collective-permute-start.6 = (f32[4,15,32,128]{3,2,1,0:T(8,128)}, f32[4,15,32,128]{3,2,1,0:T(8,128)}, u32[]{:S(2)}, u32[]{:S(2)}) collective-permute-start(f32[4,15,32,128]{3,2,1,0:T(8,128)} %get-tuple-element.34), channel_id=1, source_target_pairs={{0,16},{1,17},{2,18},{3,19},{4,20},{5,21},{6,22},{7,23},{8,24},{9,... | collective-permute-start | bytes 2949128 | tf_op jit(solution)/shard_map/ppermute | solution.py:15
  116.2 17.9 %collective-permute-done.6 = f32[4,15,32,128]{3,2,1,0:T(8,128)} collective-permute-done((f32[4,15,32,128]{3,2,1,0:T(8,128)}, f32[4,15,32,128]{3,2,1,0:T(8,128)}, u32[]{:S(2)}, u32[]{:S(2)}) %collective-permute-start.6) | collective-permute-done | bytes 983072 | tf_op jit(solution)/shard_map/ppermute | solution.py:15
  134.1 4.8 %collective-permute-done.7 = f32[4,15,32,128]{3,2,1,0:T(8,128)} collective-permute-done((f32[4,15,32,128]{3,2,1,0:T(8,128)}, f32[4,15,32,128]{3,2,1,0:T(8,128)}, u32[]{:S(2)}, u32[]{:S(2)}) %collective-permute-start.7) | collective-permute-done | bytes 983072 | tf_op jit(solution)/shard_map/ppermute | solution.py:18
  140.7 3.9 %fusion.2 = f32[4,24,32,128]{3,1,2,0:T(8,128)S(1)} fusion(f32[4,54,32,128]{3,2,1,0:T(8,128)S(1)} %pad_maximum_fusion, f32[4,54,24,1]{1,0,2,3:T(4,128)S(1)} %convolution_bitcast_fusion.3), kind=kOutput, calls=%fused_computation.2 | convolution fusion | flops 254803968 | bytes 5132544 | tf_op jit(solution)/shard_map/vjyz,vji->viyz/dot_general | solution.py:31
  145.9 3.6 collective-permute-start.8
  153.1 5.1 %collective-permute-done.8 = f32[4,24,15,128]{3,1,2,0:T(8,128)} collective-permute-done((f32[4,24,15,128]{3,1,2,0:T(8,128)}, f32[4,24,15,128]{3,1,2,0:T(8,128)}, u32[]{:S(2)}, u32[]{:S(2)}) %collective-permute-start.8) | collective-permute-done | bytes 737312 | tf_op jit(solution)/shard_map/ppermute | solution.py:15
  158.2 4.4 %collective-permute-done.9 = f32[4,24,15,128]{3,1,2,0:T(8,128)} collective-permute-done((f32[4,24,15,128]{3,1,2,0:T(8,128)}, f32[4,24,15,128]{3,1,2,0:T(8,128)}, u32[]{:S(2)}, u32[]{:S(2)}) %collective-permute-start.9) | collective-permute-done | bytes 737312 | tf_op jit(solution)/shard_map/ppermute | solution.py:18
  168.6 2.9 copy.45
  171.5 3.8 collective-permute-start.10
  175.4 2.9 copy.46
  186.4 5.0 %collective-permute-done.11 = f32[4,24,32,15]{2,1,3,0:T(8,128)} collective-permute-done((f32[4,24,32,15]{2,1,3,0:T(8,128)}, f32[4,24,32,15]{2,1,3,0:T(8,128)}, u32[]{:S(2)}, u32[]{:S(2)}) %collective-permute-start.11) | collective-permute-done | bytes 184352 | tf_op jit(solution)/shard_map/ppermute | solution.py:18
  194.2 5.7 %fusion.58 = f32[24,32,128]{2,1,0:T(8,128)S(1)} fusion(f32[24,32,128]{2,1,0:T(8,128)} %param.4, f32[4,24,32,15]{3,2,1,0:T(8,128)} %copy.48, f32[4,24,32,128]{3,2,1,0:T(8,128)S(1)} %fusion.41, f32[4,24,32,15]{3,2,1,0:T(8,128)} %copy.47, f32[4,158,128,1]{2,0,1,3:T(4,128)} %fusion.66), kind=kOutput, calls=%fused_computation.60 | convolution fusion | flops 746606592 | bytes 3051520 | tf_op jit(solution)/shard_map/vxyj,vji->xyi/dot_general | solution.py:31
  204.4 3.8 collective-permute-done.13
  210.2 4.0 %collective-permute-start.14 = (f32[4,24,15,128]{3,1,2,0:T(8,128)S(1)}, f32[4,24,15,128]{3,1,2,0:T(8,128)S(1)}, u32[]{:S(2)}, u32[]{:S(2)}) collective-permute-start(f32[4,24,15,128]{3,1,2,0:T(8,128)S(1)} %get-tuple-element.28), channel_id=1, source_target_pairs={{0,4},{4,8},{8,12},{1,5},{5,9},{9,13},{2,6},{6,10},{10,14},{3,7},{... | collective-permute-start | bytes 2211848 | tf_op jit(solution)/shard_map/ppermute | solution.py:15
  216.5 6.1 %collective-permute-done.14 = f32[4,24,15,128]{3,1,2,0:T(8,128)S(1)} collective-permute-done((f32[4,24,15,128]{3,1,2,0:T(8,128)S(1)}, f32[4,24,15,128]{3,1,2,0:T(8,128)S(1)}, u32[]{:S(2)}, u32[]{:S(2)}) %collective-permute-start.14) | collective-permute-done | bytes 737312 | tf_op jit(solution)/shard_map/ppermute | solution.py:15
  222.6 4.5 %collective-permute-done.15 = f32[4,24,15,128]{3,1,2,0:T(8,128)S(1)} collective-permute-done((f32[4,24,15,128]{3,1,2,0:T(8,128)S(1)}, f32[4,24,15,128]{3,1,2,0:T(8,128)S(1)}, u32[]{:S(2)}, u32[]{:S(2)}) %collective-permute-start.15) | collective-permute-done | bytes 737312 | tf_op jit(solution)/shard_map/ppermute | solution.py:18
  231.8 2.9 copy.55
  237.0 2.9 copy.56
  241.2 3.6 collective-permute-done.16
  247.8 4.7 %collective-permute-done.17 = f32[4,24,32,15]{2,1,3,0:T(8,128)} collective-permute-done((f32[4,24,32,15]{2,1,3,0:T(8,128)}, f32[4,24,32,15]{2,1,3,0:T(8,128)}, u32[]{:S(2)}, u32[]{:S(2)}) %collective-permute-start.17) | collective-permute-done | bytes 184352 | tf_op jit(solution)/shard_map/ppermute | solution.py:18
  255.4 7.1 %multiply_reduce_fusion.1 = (f32[4]{0:T(128)S(1)}, f32[4]{0:T(128)}, f32[4]{0:T(128)}, f32[4,24,32,128]{3,2,1,0:T(8,128)}) fusion(f32[4,24,32,128]{3,2,1,0:T(8,128)S(1)} %copy-done, f32[4,158,128,1]{2,0,1,3:T(4,128)} %copy-done.1, f32[4,24,32,15]{3,2,1,0:T(8,128)} %copy.58, f32[4,24,32,128]{3,2,1,0:T(8,128)S(1)} %fusion.44, f32[4,24,32,15]{3,2,1,0:T(8,128)} %copy.57), kind=kOutput, calls=%fused_computation.46 | convolution fusion | flops 748474368 | bytes 5410864 | tf_op jit(solution)/shard_map/vxyj,vji->vxyi/dot_general | solution.py:31
  262.4 36.9 %all-reduce = (f32[4]{0:T(128)S(1)}, f32[4]{0:T(128)S(1)}, f32[4]{0:T(128)S(1)}, f32[4]{0:T(128)S(1)}, f32[4]{0:T(128)S(1)}, /*index=5*/f32[4]{0:T(128)S(1)}) all-reduce(f32[4]{0:T(128)} %get-tuple-element.9, f32[4]{0:T(128)S(1)} %copy-done.13, f32[4]{0:T(128)} %get-tuple-element.8, ...), channel_id=1, replica_groups=mesh['gx'=2,'gy'=4,'gz'=4] {'gx','gy','gz'}, use_global_device_ids=true, to_apply=%region_8.0 | all-reduce | flops 24 | bytes 192 | tf_op jit(solution)/shard_map/psum | solution.py:62
  302.1 4.4 %collective-permute-start.18 = (f32[4,15,32,128]{3,2,1,0:T(8,128)S(1)}, f32[4,15,32,128]{3,2,1,0:T(8,128)S(1)}, u32[]{:S(2)}, u32[]{:S(2)}) collective-permute-start(f32[4,15,32,128]{3,2,1,0:T(8,128)S(1)} %get-tuple-element.24), channel_id=1, source_target_pairs={{0,16},{1,17},{2,18},{3,19},{4,20},{5,21},{6,22},{7,23},{8,24},{9,... | collective-permute-start | bytes 2949128 | tf_op jit(solution)/shard_map/ppermute | solution.py:15
  308.2 18.3 %collective-permute-done.18 = f32[4,15,32,128]{3,2,1,0:T(8,128)S(1)} collective-permute-done((f32[4,15,32,128]{3,2,1,0:T(8,128)S(1)}, f32[4,15,32,128]{3,2,1,0:T(8,128)S(1)}, u32[]{:S(2)}, u32[]{:S(2)}) %collective-permute-start.18) | collective-permute-done | bytes 983072 | tf_op jit(solution)/shard_map/ppermute | solution.py:15
  326.5 4.0 %collective-permute-done.19 = f32[4,15,32,128]{3,2,1,0:T(8,128)S(1)} collective-permute-done((f32[4,15,32,128]{3,2,1,0:T(8,128)S(1)}, f32[4,15,32,128]{3,2,1,0:T(8,128)S(1)}, u32[]{:S(2)}, u32[]{:S(2)}) %collective-permute-start.19) | collective-permute-done | bytes 983072 | tf_op jit(solution)/shard_map/ppermute | solution.py:18
  331.0 3.9 %fusion = f32[4,24,32,128]{3,1,2,0:T(8,128)S(1)} fusion(f32[4,54,32,128]{3,2,1,0:T(8,128)S(1)} %pad_maximum_fusion.1, f32[4,54,24,1]{1,0,2,3:T(4,128)S(1)} %copy-done.7), kind=kOutput, calls=%fused_computation | convolution fusion | flops 254803968 | bytes 5132544 | tf_op jit(solution)/shard_map/vjyz,vji->viyz/dot_general | solution.py:31
  335.0 3.8 collective-permute-start.20
  340.8 6.3 %collective-permute-done.20 = f32[4,24,15,128]{3,1,2,0:T(8,128)S(1)} collective-permute-done((f32[4,24,15,128]{3,1,2,0:T(8,128)S(1)}, f32[4,24,15,128]{3,1,2,0:T(8,128)S(1)}, u32[]{:S(2)}, u32[]{:S(2)}) %collective-permute-start.20) | collective-permute-done | bytes 737312 | tf_op jit(solution)/shard_map/ppermute | solution.py:15
  347.1 4.5 %collective-permute-done.21 = f32[4,24,15,128]{3,1,2,0:T(8,128)S(1)} collective-permute-done((f32[4,24,15,128]{3,1,2,0:T(8,128)S(1)}, f32[4,24,15,128]{3,1,2,0:T(8,128)S(1)}, u32[]{:S(2)}, u32[]{:S(2)}) %collective-permute-start.21) | collective-permute-done | bytes 737312 | tf_op jit(solution)/shard_map/ppermute | solution.py:18
  355.8 3.0 copy.64
  358.8 3.8 collective-permute-start.22
  366.3 4.1 %collective-permute-done.22 = f32[4,24,32,15]{2,1,3,0:T(8,128)} collective-permute-done((f32[4,24,32,15]{2,1,3,0:T(8,128)}, f32[4,24,32,15]{2,1,3,0:T(8,128)}, u32[]{:S(2)}, u32[]{:S(2)}) %collective-permute-start.22) | collective-permute-done | bytes 184352 | tf_op jit(solution)/shard_map/ppermute | solution.py:15
  372.2 4.5 %collective-permute-done.23 = f32[4,24,32,15]{2,1,3,0:T(8,128)} collective-permute-done((f32[4,24,32,15]{2,1,3,0:T(8,128)}, f32[4,24,32,15]{2,1,3,0:T(8,128)}, u32[]{:S(2)}, u32[]{:S(2)}) %collective-permute-start.23) | collective-permute-done | bytes 184352 | tf_op jit(solution)/shard_map/ppermute | solution.py:18
  376.7 2.9 copy.67
  379.6 5.8 %fusion.61 = f32[24,32,128]{2,1,0:T(8,128)} fusion(f32[24,32,128]{2,1,0:T(8,128)S(1)} %fusion.58, f32[4,24,32,15]{3,2,1,0:T(8,128)} %copy.67, f32[4,24,32,128]{3,2,1,0:T(8,128)S(1)} %fusion.47, f32[4,24,32,15]{3,2,1,0:T(8,128)S(1)} %copy.66, f32[4,158,128,1]{2,0,1,3:T(4,128)} %fusion.66), kind=kOutput, calls=%fused_computation.61 | convolution fusion | flops 746606592 | bytes 3051520 | tf_op jit(solution)/shard_map/vxyj,vji->xyi/dot_general | solution.py:31
  (107 shorter events, 85.7 us)
Async XLA Ops:
  0.6 6.5 %copy-start.12 = (s32[4,3,31]{2,0,1:T(4,128)S(1)}, s32[4,3,31]{2,0,1:T(4,128)}, u32[]{:S(2)}) copy-start(s32[4,3,31]{2,0,1:T(4,128)} %param.6) | copy-start | bytes 4468
  1.9 8.9 %collective-permute-start = (f32[15,32,128]{2,0,1:T(8,128)S(1)}, f32[15,32,128]{2,0,1:T(8,128)S(1)}, u32[]{:S(2)}, u32[]{:S(2)}) collective-permute-start(f32[15,32,128]{2,0,1:T(8,128)S(1)} %get-tuple-element.42), channel_id=1, source_target_pairs={{0,16},{1,17},{2,18},{3,19},{4,20},{5,21},{6,22},{7,23},{8,24},{9,... | collective-permute-start | bytes 737288 | tf_op jit(solution)/shard_map/ppermute | solution.py:15
  5.9 8.8 %collective-permute-start.1 = (f32[15,32,128]{2,0,1:T(8,128)S(1)}, f32[15,32,128]{2,0,1:T(8,128)S(1)}, u32[]{:S(2)}, u32[]{:S(2)}) collective-permute-start(f32[15,32,128]{2,0,1:T(8,128)S(1)} %get-tuple-element.43), channel_id=1, source_target_pairs={{16,0},{17,1},{18,2},{19,3},{20,4},{21,5},{22,6},{23,7},{24,8},{25... | collective-permute-start | bytes 737288 | tf_op jit(solution)/shard_map/ppermute | solution.py:18
  7.5 7.2 %copy-start.8 = (f32[4,54,24,1]{1,0,2,3:T(4,128)}, f32[4,54,24,1]{1,0,2,3:T(4,128)S(1)}, u32[]{:S(2)}) copy-start(f32[4,54,24,1]{1,0,2,3:T(4,128)S(1)} %convolution_bitcast_fusion.2) | copy-start | bytes 62212
  16.2 13.2 %collective-permute-start.2 = (f32[4,24,15,128]{3,1,2,0:T(8,128)S(1)}, f32[4,24,15,128]{3,1,2,0:T(8,128)S(1)}, u32[]{:S(2)}, u32[]{:S(2)}) collective-permute-start(f32[4,24,15,128]{3,1,2,0:T(8,128)S(1)} %get-tuple-element.38), channel_id=1, source_target_pairs={{0,4},{4,8},{8,12},{1,5},{5,9},{9,13},{2,6},{6,10},{10,14},{3,7},{... | collective-permute-start | bytes 2211848 | tf_op jit(solution)/shard_map/ppermute | solution.py:15
  21.0 12.8 %collective-permute-start.3 = (f32[4,24,15,128]{3,1,2,0:T(8,128)S(1)}, f32[4,24,15,128]{3,1,2,0:T(8,128)S(1)}, u32[]{:S(2)}, u32[]{:S(2)}) collective-permute-start(f32[4,24,15,128]{3,1,2,0:T(8,128)S(1)} %get-tuple-element.39), channel_id=1, source_target_pairs={{4,0},{8,4},{12,8},{5,1},{9,5},{13,9},{6,2},{10,6},{14,10},{7,3},{... | collective-permute-start | bytes 2211848 | tf_op jit(solution)/shard_map/ppermute | solution.py:18
  23.3 10.8 %copy-start.4 = (f32[4,62,32,1]{1,0,2,3:T(4,128)}, f32[4,62,32,1]{1,0,2,3:T(4,128)S(1)}, u32[]{:S(2)}) copy-start(f32[4,62,32,1]{1,0,2,3:T(4,128)S(1)} %convolution_bitcast_fusion) | copy-start | bytes 95236
  40.9 11.9 %collective-permute-start.4 = (f32[4,24,32,15]{2,1,3,0:T(8,128)}, f32[4,24,32,15]{2,1,3,0:T(8,128)}, u32[]{:S(2)}, u32[]{:S(2)}) collective-permute-start(f32[4,24,32,15]{2,1,3,0:T(8,128)} %copy.36), channel_id=1, source_target_pairs={{0,1},{1,2},{2,3},{4,5},{5,6},{6,7},{8,9},{9,10},{10,11},{12,13},{... | collective-permute-start | bytes 552968 | tf_op jit(solution)/shard_map/ppermute | solution.py:15
  46.6 12.5 %collective-permute-start.5 = (f32[4,24,32,15]{2,1,3,0:T(8,128)}, f32[4,24,32,15]{2,1,3,0:T(8,128)}, u32[]{:S(2)}, u32[]{:S(2)}) collective-permute-start(f32[4,24,32,15]{2,1,3,0:T(8,128)} %copy.37), channel_id=1, source_target_pairs={{1,0},{2,1},{3,2},{5,4},{6,5},{7,6},{9,8},{10,9},{11,10},{13,12},{... | collective-permute-start | bytes 552968 | tf_op jit(solution)/shard_map/ppermute | solution.py:18
  48.4 4.4 %copy-start.10 = (s32[158,128]{1,0:T(8,128)}, s32[158,128]{1,0:T(8,128)S(1)}, u32[]{:S(2)}) copy-start(s32[158,128]{1,0:T(8,128)S(1)} %iota_subtract_fusion) | copy-start | bytes 242692
  49.3 12.7 %copy-start.1 = (f32[4,158,128,1]{2,0,1,3:T(4,128)}, f32[4,158,128,1]{2,0,1,3:T(4,128)S(1)}, u32[]{:S(2)}) copy-start(f32[4,158,128,1]{2,0,1,3:T(4,128)S(1)} %fusion.64) | copy-start | bytes 970756
  55.8 6.2 %copy-start = (f32[4,24,32,128]{3,2,1,0:T(8,128)S(1)}, f32[4,24,32,128]{3,2,1,0:T(8,128)}, u32[]{:S(2)}) copy-start(f32[4,24,32,128]{3,2,1,0:T(8,128)} %param.5) | copy-start | bytes 4718596
  105.9 1.8 copy-start.15
  105.9 1.9 copy-start.14
  109.3 24.8 %collective-permute-start.6 = (f32[4,15,32,128]{3,2,1,0:T(8,128)}, f32[4,15,32,128]{3,2,1,0:T(8,128)}, u32[]{:S(2)}, u32[]{:S(2)}) collective-permute-start(f32[4,15,32,128]{3,2,1,0:T(8,128)} %get-tuple-element.34), channel_id=1, source_target_pairs={{0,16},{1,17},{2,18},{3,19},{4,20},{5,21},{6,22},{7,23},{8,24},{9,... | collective-permute-start | bytes 2949128 | tf_op jit(solution)/shard_map/ppermute | solution.py:15
  114.6 24.3 %collective-permute-start.7 = (f32[4,15,32,128]{3,2,1,0:T(8,128)}, f32[4,15,32,128]{3,2,1,0:T(8,128)}, u32[]{:S(2)}, u32[]{:S(2)}) collective-permute-start(f32[4,15,32,128]{3,2,1,0:T(8,128)} %get-tuple-element.35), channel_id=1, source_target_pairs={{16,0},{17,1},{18,2},{19,3},{20,4},{21,5},{22,6},{23,7},{24,8},{25... | collective-permute-start | bytes 2949128 | tf_op jit(solution)/shard_map/ppermute | solution.py:18
  116.2 24.5 %copy-start.6 = (f32[4,54,24,1]{1,0,2,3:T(4,128)}, f32[4,54,24,1]{1,0,2,3:T(4,128)S(1)}, u32[]{:S(2)}) copy-start(f32[4,54,24,1]{1,0,2,3:T(4,128)S(1)} %convolution_bitcast_fusion.3) | copy-start | bytes 62212
  144.6 7.6 %copy-start.16 = (s32[4]{0:T(128)S(1)}, s32[4]{0:T(128)}, u32[]{:S(2)}) copy-start(s32[4]{0:T(128)} %param.7) | copy-start | bytes 52
  145.9 12.3 %collective-permute-start.8 = (f32[4,24,15,128]{3,1,2,0:T(8,128)}, f32[4,24,15,128]{3,1,2,0:T(8,128)}, u32[]{:S(2)}, u32[]{:S(2)}) collective-permute-start(f32[4,24,15,128]{3,1,2,0:T(8,128)} %get-tuple-element.32), channel_id=1, source_target_pairs={{0,4},{4,8},{8,12},{1,5},{5,9},{9,13},{2,6},{6,10},{10,14},{3,7},{... | collective-permute-start | bytes 2211848 | tf_op jit(solution)/shard_map/ppermute | solution.py:15
  149.5 13.1 %collective-permute-start.9 = (f32[4,24,15,128]{3,1,2,0:T(8,128)}, f32[4,24,15,128]{3,1,2,0:T(8,128)}, u32[]{:S(2)}, u32[]{:S(2)}) collective-permute-start(f32[4,24,15,128]{3,1,2,0:T(8,128)} %get-tuple-element.33), channel_id=1, source_target_pairs={{4,0},{8,4},{12,8},{5,1},{9,5},{13,9},{6,2},{10,6},{14,10},{7,3},{... | collective-permute-start | bytes 2211848 | tf_op jit(solution)/shard_map/ppermute | solution.py:18
  153.1 11.0 %copy-start.2 = (f32[4,62,32,1]{1,0,2,3:T(4,128)}, f32[4,62,32,1]{1,0,2,3:T(4,128)S(1)}, u32[]{:S(2)}) copy-start(f32[4,62,32,1]{1,0,2,3:T(4,128)S(1)} %convolution_bitcast_fusion.1) | copy-start | bytes 95236
  171.5 8.1 %copy-start.17 = (s32[4]{0:T(128)S(1)}, s32[4]{0:T(128)}, u32[]{:S(2)}) copy-start(s32[4]{0:T(128)} %param.7) | copy-start | bytes 52
  171.5 8.7 %copy-start.11 = (s32[158,128]{1,0:T(8,128)S(1)}, s32[158,128]{1,0:T(8,128)}, u32[]{:S(2)}) copy-start(s32[158,128]{1,0:T(8,128)} %copy-done.10) | copy-start | bytes 242692
  171.5 11.9 %collective-permute-start.10 = (f32[4,24,32,15]{2,1,3,0:T(8,128)}, f32[4,24,32,15]{2,1,3,0:T(8,128)}, u32[]{:S(2)}, u32[]{:S(2)}) collective-permute-start(f32[4,24,32,15]{2,1,3,0:T(8,128)} %copy.45), channel_id=1, source_target_pairs={{0,1},{1,2},{2,3},{4,5},{5,6},{6,7},{8,9},{9,10},{10,11},{12,13},{... | collective-permute-start | bytes 552968 | tf_op jit(solution)/shard_map/ppermute | solution.py:15
  178.3 13.0 %collective-permute-start.11 = (f32[4,24,32,15]{2,1,3,0:T(8,128)}, f32[4,24,32,15]{2,1,3,0:T(8,128)}, u32[]{:S(2)}, u32[]{:S(2)}) collective-permute-start(f32[4,24,32,15]{2,1,3,0:T(8,128)} %copy.46), channel_id=1, source_target_pairs={{1,0},{2,1},{3,2},{5,4},{6,5},{7,6},{9,8},{10,9},{11,10},{13,12},{... | collective-permute-start | bytes 552968 | tf_op jit(solution)/shard_map/ppermute | solution.py:18
  199.9 8.4 %copy-start.9 = (f32[4,54,24,1]{1,0,2,3:T(4,128)S(1)}, f32[4,54,24,1]{1,0,2,3:T(4,128)}, u32[]{:S(2)}) copy-start(f32[4,54,24,1]{1,0,2,3:T(4,128)} %copy-done.8) | copy-start | bytes 62212
  200.0 4.4 %collective-permute-start.12 = (f32[15,32,128]{2,1,0:T(8,128)S(1)}, f32[15,32,128]{2,1,0:T(8,128)S(1)}, u32[]{:S(2)}, u32[]{:S(2)}) collective-permute-start(f32[15,32,128]{2,1,0:T(8,128)S(1)} %get-tuple-element.40), channel_id=1, source_target_pairs={{0,16},{1,17},{2,18},{3,19},{4,20},{5,21},{6,22},{7,23},{8,24},{9,... | collective-permute-start | bytes 737288 | tf_op jit(solution)/shard_map/ppermute | solution.py:15
  201.3 6.9 %collective-permute-start.13 = (f32[15,32,128]{2,1,0:T(8,128)S(1)}, f32[15,32,128]{2,1,0:T(8,128)S(1)}, u32[]{:S(2)}, u32[]{:S(2)}) collective-permute-start(f32[15,32,128]{2,1,0:T(8,128)S(1)} %get-tuple-element.41), channel_id=1, source_target_pairs={{16,0},{17,1},{18,2},{19,3},{20,4},{21,5},{22,6},{23,7},{24,8},{25... | collective-permute-start | bytes 737288 | tf_op jit(solution)/shard_map/ppermute | solution.py:18
  210.2 12.4 %collective-permute-start.14 = (f32[4,24,15,128]{3,1,2,0:T(8,128)S(1)}, f32[4,24,15,128]{3,1,2,0:T(8,128)S(1)}, u32[]{:S(2)}, u32[]{:S(2)}) collective-permute-start(f32[4,24,15,128]{3,1,2,0:T(8,128)S(1)} %get-tuple-element.28), channel_id=1, source_target_pairs={{0,4},{4,8},{8,12},{1,5},{5,9},{9,13},{2,6},{6,10},{10,14},{3,7},{... | collective-permute-start | bytes 2211848 | tf_op jit(solution)/shard_map/ppermute | solution.py:15
  214.2 13.1 %copy-start.5 = (f32[4,62,32,1]{1,0,2,3:T(4,128)S(1)}, f32[4,62,32,1]{1,0,2,3:T(4,128)}, u32[]{:S(2)}) copy-start(f32[4,62,32,1]{1,0,2,3:T(4,128)} %copy-done.4) | copy-start | bytes 95236
  214.2 12.9 %collective-permute-start.15 = (f32[4,24,15,128]{3,1,2,0:T(8,128)S(1)}, f32[4,24,15,128]{3,1,2,0:T(8,128)S(1)}, u32[]{:S(2)}, u32[]{:S(2)}) collective-permute-start(f32[4,24,15,128]{3,1,2,0:T(8,128)S(1)} %get-tuple-element.29), channel_id=1, source_target_pairs={{4,0},{8,4},{12,8},{5,1},{9,5},{13,9},{6,2},{10,6},{14,10},{7,3},{... | collective-permute-start | bytes 2211848 | tf_op jit(solution)/shard_map/ppermute | solution.py:18
  234.7 10.1 %collective-permute-start.16 = (f32[4,24,32,15]{2,1,3,0:T(8,128)}, f32[4,24,32,15]{2,1,3,0:T(8,128)}, u32[]{:S(2)}, u32[]{:S(2)}) collective-permute-start(f32[4,24,32,15]{2,1,3,0:T(8,128)} %copy.55), channel_id=1, source_target_pairs={{0,1},{1,2},{2,3},{4,5},{5,6},{6,7},{8,9},{9,10},{10,11},{12,13},{... | collective-permute-start | bytes 552968 | tf_op jit(solution)/shard_map/ppermute | solution.py:15
  239.9 12.5 %collective-permute-start.17 = (f32[4,24,32,15]{2,1,3,0:T(8,128)}, f32[4,24,32,15]{2,1,3,0:T(8,128)}, u32[]{:S(2)}, u32[]{:S(2)}) collective-permute-start(f32[4,24,32,15]{2,1,3,0:T(8,128)} %copy.56), channel_id=1, source_target_pairs={{1,0},{2,1},{3,2},{5,4},{6,5},{7,6},{9,8},{10,9},{11,10},{13,12},{... | collective-permute-start | bytes 552968 | tf_op jit(solution)/shard_map/ppermute | solution.py:18
  255.4 7.1 %copy-start.13 = (f32[4]{0:T(128)S(1)}, f32[4]{0:T(128)}, u32[]{:S(2)}) copy-start(f32[4]{0:T(128)} %get-tuple-element.5) | copy-start | bytes 52
  302.1 24.4 %collective-permute-start.18 = (f32[4,15,32,128]{3,2,1,0:T(8,128)S(1)}, f32[4,15,32,128]{3,2,1,0:T(8,128)S(1)}, u32[]{:S(2)}, u32[]{:S(2)}) collective-permute-start(f32[4,15,32,128]{3,2,1,0:T(8,128)S(1)} %get-tuple-element.24), channel_id=1, source_target_pairs={{0,16},{1,17},{2,18},{3,19},{4,20},{5,21},{6,22},{7,23},{8,24},{9,... | collective-permute-start | bytes 2949128 | tf_op jit(solution)/shard_map/ppermute | solution.py:15
  306.5 24.5 %copy-start.7 = (f32[4,54,24,1]{1,0,2,3:T(4,128)S(1)}, f32[4,54,24,1]{1,0,2,3:T(4,128)}, u32[]{:S(2)}) copy-start(f32[4,54,24,1]{1,0,2,3:T(4,128)} %copy-done.6) | copy-start | bytes 62212
  306.5 24.0 %collective-permute-start.19 = (f32[4,15,32,128]{3,2,1,0:T(8,128)S(1)}, f32[4,15,32,128]{3,2,1,0:T(8,128)S(1)}, u32[]{:S(2)}, u32[]{:S(2)}) collective-permute-start(f32[4,15,32,128]{3,2,1,0:T(8,128)S(1)} %get-tuple-element.25), channel_id=1, source_target_pairs={{16,0},{17,1},{18,2},{19,3},{20,4},{21,5},{22,6},{23,7},{24,8},{25... | collective-permute-start | bytes 2949128 | tf_op jit(solution)/shard_map/ppermute | solution.py:18
  335.0 12.2 %collective-permute-start.20 = (f32[4,24,15,128]{3,1,2,0:T(8,128)S(1)}, f32[4,24,15,128]{3,1,2,0:T(8,128)S(1)}, u32[]{:S(2)}, u32[]{:S(2)}) collective-permute-start(f32[4,24,15,128]{3,1,2,0:T(8,128)S(1)} %get-tuple-element.22), channel_id=1, source_target_pairs={{0,4},{4,8},{8,12},{1,5},{5,9},{9,13},{2,6},{6,10},{10,14},{3,7},{... | collective-permute-start | bytes 2211848 | tf_op jit(solution)/shard_map/ppermute | solution.py:15
  338.8 13.1 %copy-start.3 = (f32[4,62,32,1]{1,0,2,3:T(4,128)S(1)}, f32[4,62,32,1]{1,0,2,3:T(4,128)}, u32[]{:S(2)}) copy-start(f32[4,62,32,1]{1,0,2,3:T(4,128)} %copy-done.2) | copy-start | bytes 95236
  338.8 12.9 %collective-permute-start.21 = (f32[4,24,15,128]{3,1,2,0:T(8,128)S(1)}, f32[4,24,15,128]{3,1,2,0:T(8,128)S(1)}, u32[]{:S(2)}, u32[]{:S(2)}) collective-permute-start(f32[4,24,15,128]{3,1,2,0:T(8,128)S(1)} %get-tuple-element.23), channel_id=1, source_target_pairs={{4,0},{8,4},{12,8},{5,1},{9,5},{13,9},{6,2},{10,6},{14,10},{7,3},{... | collective-permute-start | bytes 2211848 | tf_op jit(solution)/shard_map/ppermute | solution.py:18
  358.8 11.6 %collective-permute-start.22 = (f32[4,24,32,15]{2,1,3,0:T(8,128)}, f32[4,24,32,15]{2,1,3,0:T(8,128)}, u32[]{:S(2)}, u32[]{:S(2)}) collective-permute-start(f32[4,24,32,15]{2,1,3,0:T(8,128)} %copy.64), channel_id=1, source_target_pairs={{0,1},{1,2},{2,3},{4,5},{5,6},{6,7},{8,9},{9,10},{10,11},{12,13},{... | collective-permute-start | bytes 552968 | tf_op jit(solution)/shard_map/ppermute | solution.py:15
  364.2 12.5 %collective-permute-start.23 = (f32[4,24,32,15]{2,1,3,0:T(8,128)}, f32[4,24,32,15]{2,1,3,0:T(8,128)}, u32[]{:S(2)}, u32[]{:S(2)}) collective-permute-start(f32[4,24,32,15]{2,1,3,0:T(8,128)} %copy.65), channel_id=1, source_target_pairs={{1,0},{2,1},{3,2},{5,4},{6,5},{7,6},{9,8},{10,9},{11,10},{13,12},{... | collective-permute-start | bytes 552968 | tf_op jit(solution)/shard_map/ppermute | solution.py:18
where the time goes:
time: 392 us; the launch traced here: 386 us
  waiting for transfers between devices  130 us (33%)
  blocking collectives  73.7 us (19%)
  starting transfers between devices  65.6 us (17%)
  local copies, waits for them, and re-layouts  55.7 us (14%)
  matrix products  48.9 us (12%)
  other arithmetic  10.7 us (3%)
    ppermute x12, waiting for transfers between devices, extended(): lax.ppermute(lax.slice_in_dim(block, block.shape[dim] - width, None, axis...  77.7 us
    ppermute x12, waiting for transfers between devices, extended(): lax.ppermute(lax.slice_in_dim(block, 0, width, axis=dim), axis, backward)  51.9 us
    dot_general x12, matrix products, product(): return jnp.einsum(form, left, right, precision=lax.Precision.HIGHEST)  45.4 us
    ppermute x12, starting transfers between devices, extended(): lax.ppermute(lax.slice_in_dim(block, block.shape[dim] - width, None, axis...  45.2 us
    psum x1, blocking collectives, local(): lax.psum((local_total, jnp.sum(view_images * blurred, axis=(1, 2, 3)), jn...  36.9 us
    psum x1, blocking collectives, local(): lax.psum((jnp.sum(view_images, axis=(1, 2, 3)), jnp.sum(view_images * vie...  36.8 us
    slice x16, local copies, waits for them, and re-layouts, extended(): lax.slice_in_dim(block, block.shape[dim] - width, None, axis=dim)  23.2 us
    ppermute x12, starting transfers between devices, extended(): lax.ppermute(lax.slice_in_dim(block, 0, width, axis=dim), axis, backward)  20.4 us
  transfers between devices with their start and end apart: 24, of which 24 were waited for; matrix products, arithmetic and copies ran while one was open for 6% of the time, Pallas kernels for 0%

commit v1 on v0

v1 whole, which is shorter than its diff:
```python
import functools

import jax
import jax.numpy as jnp
from jax import lax
from jax.experimental import pallas as pl
from jax.experimental.pallas import tpu as pltpu
from jax.sharding import PartitionSpec as P

TAPS = 31
ITERS = 2
REACH = 15
PAD = 16
LANES = 128
MESH = pl.DeviceIdType.MESH
AXES = ("gx", "gy", "gz")
F32 = jnp.float32
BF16 = jnp.bfloat16
STATS = 5


def halves(value, axis):
    high = value.astype(BF16).astype(F32)
    return jnp.concatenate([high, value - high], axis=axis).astype(BF16)


def dot(left, right):
    return jnp.dot(left, right, preferred_element_type=F32)


def dot_nt(left, right):
    return lax.dot_general(left, right, (((1,), (1,)), ((), ())), preferred_element_type=F32)


def dot_tn(left, right):
    return lax.dot_general(left, right, (((0,), (0,)), ((), ())), preferred_element_type=F32)


def iota(shape, dim):
    return lax.broadcasted_iota(jnp.int32, shape, dim)


class Shift:
    def __init__(self, axis, count, step, source, target, send_sem, recv_sem, swap=False):
        me = lax.axis_index(axis)
        if swap:
            self.sends = self.receives = None
            goal = 1 - me
        else:
            self.sends = (me + step >= 0) & (me + step < count)
            self.receives = (me - step >= 0) & (me - step < count)
            goal = me + step
        self.copy = pltpu.make_async_remote_copy(
            src_ref=source, dst_ref=target, send_sem=send_sem, recv_sem=recv_sem,
            device_id={axis: goal}, device_id_type=MESH,
        )

    def when(self, condition, action):
        if condition is None:
            action()
        else:
            pl.when(condition)(action)

    def start(self):
        self.when(self.sends, self.copy.start)

    def wait_recv(self):
        self.when(self.receives, self.copy.wait_recv)

    def wait_send(self):
        self.when(self.sends, self.copy.wait_send)


def kernel(sizes, taps_ref, weights_ref, est_ref, images_ref, out_ref, misfit_ref,
           img, eo, eh, fo, fh, quo, uo, uh, co, ch, ts, tr, bs, br, ry, rx, yr, xr, stats, ar, ar_own, scale,
           kx, kxb, ky, kyb, kz, kzh, kzb, img_sem, send, recv, ar_send, ar_recv):
    counts, (views, nx, ny, nz) = sizes
    xs = eo.shape[2]
    ys = ny + 2 * PAD
    fstride = fo.shape[0] // (views * nx)
    ustride = uo.shape[0] // ys
    chunk = 8
    rows = chunk * ny
    blocks = nx // chunk
    flat = ys * xs
    pieces = flat // LANES
    swap = counts[0] == 2
    mx, my, mz = (lax.axis_index(a) for a in AXES)

    image_copy = pltpu.make_async_copy(images_ref, img, img_sem)
    image_copy.start()

    barrier = pltpu.get_barrier_semaphore()
    greeted = 0
    for axis, count, me in zip(AXES, counts, (mx, my, mz)):
        for p in range(1, count):
            pl.semaphore_signal(barrier, inc=1, device_id={axis: lax.rem(me + p, count)}, device_id_type=MESH)
            greeted += 1

    for y in range(ny):
        eo[0, PAD + y, 0:nx, :] = est_ref[pl.ds(y, nx, stride=ny), :]

    pl.semaphore_wait(barrier, greeted)

    own_y = pl.ds(PAD, ny)
    face = pl.multiple_of((1 - mx) * (nx - PAD), 8) if swap else None

    def x_gather(it):
        if swap:
            return [Shift("gx", 2, 1, eo.at[it, own_y, pl.ds(face, PAD), :], xr.at[it, 0],
                          send.at[it, 0], recv.at[it, 0], swap=True)]
        return [
            Shift("gx", counts[0], 1, eo.at[it, own_y, pl.ds(nx - PAD, PAD), :],
                  xr.at[it, 0], send.at[it, 0], recv.at[it, 0]),
            Shift("gx", counts[0], -1, eo.at[it, own_y, pl.ds(0, PAD), :],
                  xr.at[it, 1], send.at[it, 1], recv.at[it, 1]),
        ]

    def y_gather(it):
        return [
            Shift("gy", counts[1], 1, eo.at[it, pl.ds(ny, PAD)], yr.at[it, 0],
                  send.at[it, 2], recv.at[it, 2]),
            Shift("gy", counts[1], -1, eo.at[it, pl.ds(PAD, PAD)], yr.at[it, 1],
                  send.at[it, 3], recv.at[it, 3]),
        ]

    def z_pair(it, source, target, first):
        return [
            Shift("gz", counts[2], 1, source.at[it, pl.ds(PAD, PAD)], target.at[it, pl.ds(0, PAD)],
                  send.at[it, first], recv.at[it, first]),
            Shift("gz", counts[2], -1, source.at[it, pl.ds(0, PAD)], target.at[it, pl.ds(PAD, PAD)],
                  send.at[it, first + 1], recv.at[it, first + 1]),
        ]

    def y_reduce(it):
        return [
            Shift("gy", counts[1], 1, co.at[it, pl.ds(PAD + ny, PAD)], ry.at[it, 0],
                  send.at[it, 8], recv.at[it, 8]),
            Shift("gy", counts[1], -1, co.at[it, pl.ds(0, PAD)], ry.at[it, 1],
                  send.at[it, 9], recv.at[it, 9]),
        ]

    def x_reduce(it):
        if swap:
            return [Shift("gx", 2, 1, co.at[it, own_y, pl.ds(nx, PAD), :], rx.at[it, 0],
                          send.at[it, 10], recv.at[it, 10], swap=True)]
        return [
            Shift("gx", counts[0], 1, co.at[it, own_y, pl.ds(nx + PAD, PAD), :], rx.at[it, 0],
                  send.at[it, 10], recv.at[it, 10]),
            Shift("gx", counts[0], -1, co.at[it, own_y, pl.ds(nx, PAD), :], rx.at[it, 1],
                  send.at[it, 11], recv.at[it, 11]),
        ]

    def start(copies):
        for c in copies:
            c.start()
        return copies

    def arrive(copies):
        for c in copies:
            c.wait_recv()
            c.wait_send()

    gathers = start(x_gather(0))

    def edges():
        def clear(condition, ref, index):
            @pl.when(condition)
            def _():
                ref[index] = jnp.zeros(ref.at[index].shape, F32)
        for it in range(ITERS):
            clear(my == 0, yr, (it, 0))
            clear(my == counts[1] - 1, yr, (it, 1))
            clear(my == 0, ry, (it, 0))
            clear(my == counts[1] - 1, ry, (it, 1))
            for ref in (tr, br):
                clear(mz == 0, ref, (it, pl.ds(0, PAD)))
                clear(mz == counts[2] - 1, ref, (it, pl.ds(PAD, PAD)))
            if not swap:
                clear(mx == 0, xr, (it, 0))
                clear(mx == counts[0] - 1, xr, (it, 1))
                clear(mx == 0, rx, (it, 0))
                clear(mx == counts[0] - 1, rx, (it, 1))

    edges()

    def x_position(slot):
        if swap:
            return jnp.where(slot < nx, slot, slot - jnp.where(mx == 0, 0, nx + PAD))
        return jnp.where(slot < nx, slot, jnp.where(slot < nx + PAD, slot - nx - PAD, slot - PAD))

    def z_position(slot):
        position = jnp.where(slot < PAD, slot - PAD, slot - PAD + nz)
        return jnp.where(slot < 2 * PAD, position, -nz * 4)

    def fill(view, dim, offsets):
        def step(t, total):
            tap = taps_ref[view, dim, t].astype(F32) * (1.0 / 256.0)
            return tuple(jnp.where(o == t, tap, m) for o, m in zip(offsets, total))
        return lax.fori_loop(0, TAPS, step, tuple(jnp.zeros(o.shape, F32) for o in offsets), unroll=4)

    def pair(value, axis):
        return jnp.concatenate([value, value], axis=axis).astype(BF16)

    columns = []
    for v in range(views):
        f_shape, b_shape = (nx, xs), (xs, nx)
        f, b = fill(v, 0, (
            x_position(iota(f_shape, 1)) - iota(f_shape, 0) + REACH,
            x_position(iota(b_shape, 0)) - iota(b_shape, 1) + REACH,
        ))
        kx[pl.ds(v * nx, nx), 0:xs] = f
        kx[pl.ds(v * nx, nx), xs:2 * xs] = f
        columns.append(b)
        f_shape, b_shape = (ny, ys), (ys, ny)
        f, b = fill(v, 1, (
            iota(f_shape, 1) - PAD - iota(f_shape, 0) + REACH,
            iota(b_shape, 0) - PAD - iota(b_shape, 1) + REACH,
        ))
        ky[v] = pair(f, 1)
        kyb[v] = pair(b, 1)
        square = (nz, nz)
        halo = (LANES, nz)
        back = (nz, LANES)
        f, h = fill(v, 2, (
            iota(square, 0) - iota(square, 1) + REACH,
            z_position(iota(halo, 0)) - iota(halo, 1) + REACH,
        ))
        kz[v] = pair(f, 0)
        kzh[v] = pair(h, 0)
        f, b = fill(v, 2, (
            iota(square, 1) - iota(square, 0) + REACH,
            z_position(iota(back, 1)) - iota(back, 0) + REACH,
        ))
        kzb[v, :, 0:nz] = pair(f, 0)
        kzb[v, :, nz:nz + LANES] = pair(b, 0)
    kxb[...] = jnp.concatenate(columns + columns, axis=1).astype(BF16)

    picks = (2 * PAD, LANES)
    ends = jnp.where(iota(picks, 0) < PAD, iota(picks, 0), iota(picks, 0) + nz - 2 * PAD)
    pick_ends = (iota(picks, 1) == ends).astype(F32)
    pick_first = (iota(picks, 1) == iota(picks, 0)).astype(F32)
    ends_wide, first_wide = pair(pick_ends, 1), pair(pick_first, 1)
    ends_tall, first_tall = pair(pick_ends, 0), pair(pick_first, 0)

    normalizer = jnp.float32(0.0)
    for v in range(views):
        product = jnp.float32(1.0)
        for d in range(3):
            total = lax.fori_loop(0, TAPS, lambda t, s, v=v, d=d: s + taps_ref[v, d, t], jnp.int32(0))
            product = product * (total.astype(F32) * (1.0 / 256.0))
        normalizer = normalizer + weights_ref[v].astype(F32) * product

    def loop(low, high, unroll, body):
        assert (high - low) % unroll == 0
        def step(i, carry):
            for u in range(unroll):
                body(low + i * unroll + u)
            return carry
        lax.fori_loop(0, (high - low) // unroll, step, 0)

    def blur_x(source, target, low, high):
        matrix = kx[...].astype(BF16)
        def body(y):
            target[pl.ds(y, views * nx, stride=fstride), :] = dot(matrix, halves(source[y], 0))
        loop(low, high, 4, body)

    def spread_x(source, target):
        matrix = kxb[...]
        weight = scale[...]
        def body(y):
            target[y] = dot(matrix, halves(source[pl.ds(pl.multiple_of(y * ustride, 8), views * nx), :] * weight, 0))
        loop(0, ys, 4, body)

    def turned(source, target, select, it):
        per = LANES // 8
        def body(i):
            block = source[pl.ds(pl.multiple_of(i * LANES, LANES), LANES), :]
            target[it, :, pl.ds(pl.multiple_of(i * LANES, LANES), LANES)] = dot_nt(select, halves(block, 1))
        loop(0, pieces, 4, body)

    for it in range(ITERS):
        last = it == ITERS - 1
        arrive(gathers)
        for y in range(ny):
            for side in range(xr.shape[1]):
                eo[it, PAD + y, pl.ds(nx + side * PAD, PAD), :] = xr[it, side, y]
        gathers = start(y_gather(it))
        blur_x(eo.at[it], fo, PAD, PAD + ny)
        arrive(gathers)
        for y in range(PAD):
            eo[it, y] = yr[it, 0, y]
            eo[it, PAD + ny + y] = yr[it, 1, y]
        turned(eo.at[it].reshape(flat, LANES), ts, ends_wide, it)
        gathers = start(z_pair(it, ts, tr, 4))
        blur_x(eo.at[it], fo, 0, PAD)
        blur_x(eo.at[it], fo, PAD + ny, ys)
        arrive(gathers)
        flat_eh = eh.reshape(flat, LANES)
        def unturn(i):
            at = pl.ds(pl.multiple_of(i * LANES, LANES), LANES)
            flat_eh[at, :] = dot_tn(halves(tr[it, :, at], 0), first_tall)
        loop(0, pieces, 4, unturn)
        blur_x(eh, fh, 0, ys)

        if it == 0:
            image_copy.wait()
        stats[...] = jnp.zeros_like(stats)

        def forward(i, carry):
            v = i // blocks
            base = i * chunk
            own, side = [], []
            for u in range(chunk):
                at = pl.ds(pl.multiple_of((base + u) * fstride, 8), ys)
                both = jnp.concatenate([fo[at, :], fh[at, :]], axis=1)
                value = dot(ky[v], halves(both, 0))
                own.append(value[:, 0:nz])
                side.append(value[:, nz:nz + LANES])
            blurred = dot(halves(jnp.concatenate(own, axis=0), 1), kz[v])
            blurred = blurred + dot(halves(jnp.concatenate(side, axis=0), 1), kzh[v])
            at = pl.ds(pl.multiple_of(i * rows, rows), rows)
            image = img[at, :]
            quo[at, :] = image / blurred
            terms = [blurred, image * blurred, blurred * blurred, image, image * image]
            for k, term in enumerate(terms):
                folded = jnp.sum(term.reshape(rows // 8, 8, nz), axis=0)
                stats[k, v] = stats[k, v] + folded
            return carry

        lax.fori_loop(0, views * blocks, forward, 0)

        def reduce_start(a, value):
            axis, count, me = AXES[a], counts[a], (mx, my, mz)[a]
            ar_own[it, a] = value
            copies = []
            for p in range(1, count):
                c = pltpu.make_async_remote_copy(
                    src_ref=ar_own.at[it, a], dst_ref=ar.at[it, a, p - 1],
                    send_sem=ar_send.at[it, a, p - 1], recv_sem=ar_recv.at[it, a, p - 1],
                    device_id={axis: lax.rem(me + p, count)}, device_id_type=MESH,
                )
                c.start()
                copies.append(c)
            return copies

        def reduce_end(a, copies):
            for c in copies:
                c.wait()
            terms = [ar_own[it, a]] + [ar[it, a, p - 1] for p in range(1, counts[a])]
            while len(terms) > 1:
                half = len(terms) // 2
                terms = [terms[i] + terms[i + half] for i in range(half)] + terms[2 * half:]
            return terms[0]

        def backward(low, high):
            def step(i, carry):
                v = i // blocks
                at = pl.ds(pl.multiple_of(i * rows, rows), rows)
                wide = dot(halves(quo[at, :], 1), kzb[v])
                for u in range(chunk):
                    value = dot(kyb[v], halves(wide[u * ny:(u + 1) * ny], 0))
                    at = pl.ds(i * chunk + u, ys, stride=ustride)
                    uo[at, :] = value[:, 0:nz]
                    uh[at, :] = value[:, nz:nz + LANES]
                return carry
            lax.fori_loop(low, high, step, 0)

        folded = jnp.sum(stats[...], axis=2)
        parts = []
        for k in range(STATS):
            parts += [folded[k], jnp.ones((8 - views, LANES), F32)]
        total = jnp.concatenate(parts, axis=0)
        steps = views * blocks
        marks = (0, steps // 3, 2 * steps // 3, steps)
        for a in range(3):
            copies = reduce_start(a, total)
            backward(marks[a], marks[a + 1])
            total = reduce_end(a, copies)
        total = jnp.broadcast_to(jnp.sum(total, axis=1, keepdims=True), total.shape)
        blurred_total, cross, square, data_total, data_square = (total[8 * k:8 * k + 8] for k in range(STATS))
        flux = data_total / blurred_total
        misfit = (data_square - 2.0 * flux * cross + flux * flux * square) / data_square
        lane = iota(misfit.shape, 1)
        line = jnp.sum(jnp.where(lane == iota(misfit.shape, 0), misfit, 0.0), axis=0, keepdims=True)
        misfit_ref[it:it + 1, :] = line[:, 0:views]
        for v in range(views):
            top = jnp.full((1, LANES), weights_ref[v].astype(F32), F32)
            row = top / (jnp.full((1, LANES), normalizer, F32) * flux[v:v + 1])
            scale[pl.ds(v * nx, nx), :] = jnp.broadcast_to(row, (nx, LANES))

        spread_x(uh, ch)
        turned(ch.reshape(flat, LANES), bs, first_wide, it)
        gathers = start(z_pair(it, bs, br, 6))
        spread_x(uo, co.at[it])
        arrive(gathers)
        flat_co = co.at[it].reshape(flat, LANES)
        def add_z(i):
            at = pl.ds(pl.multiple_of(i * LANES, LANES), LANES)
            flat_co[at, :] = flat_co[at, :] + dot_tn(halves(br[it, :, at], 0), ends_tall)
        loop(0, pieces, 4, add_z)
        gathers = start(y_reduce(it))
        arrive(gathers)
        def add_y(i):
            co[it, PAD + i] = co[it, PAD + i] + ry[it, 0, i]
            co[it, ny + i] = co[it, ny + i] + ry[it, 1, i]
        loop(0, PAD, 4, add_y)
        gathers = start(x_reduce(it))
        arrive(gathers)
        def update(y):
            if swap:
                at = pl.ds(face, PAD)
                co[it, PAD + y, at, :] = co[it, PAD + y, at, :] + rx[it, 0, y]
            else:
                co[it, PAD + y, 0:PAD, :] = co[it, PAD + y, 0:PAD, :] + rx[it, 0, y]
                co[it, PAD + y, nx - PAD:nx, :] = co[it, PAD + y, nx - PAD:nx, :] + rx[it, 1, y]
            value = eo[it, PAD + y, 0:nx, :] * co[it, PAD + y, 0:nx, :]
            if last:
                out_ref[pl.ds(y, nx, stride=ny), :] = value
            else:
                eo[it + 1, PAD + y, 0:nx, :] = value
        loop(0, ny, 4, update)
        if not last:
            gathers = start(x_gather(it + 1))


def local(counts, estimate, view_images, psf_taps, view_weights):
    views, nx, ny, nz = view_images.shape
    sides = 1 if counts[0] == 2 else 2
    xs = nx + sides * PAD
    ys = ny + 2 * PAD
    flat = ys * xs
    vx = views * nx
    peak = max(counts)
    fstride, ustride = ys + 8, vx + 8
    vmem = pltpu.VMEM
    scratch = [
        vmem((views * nx * ny, nz), F32),
        vmem((ITERS, ys, xs, nz), F32),
        vmem((ys, xs, LANES), F32),
        vmem((vx * fstride, nz), F32),
        vmem((vx * fstride, LANES), F32),
        vmem((views * nx * ny, nz), F32),
        vmem((ys * ustride, nz), F32),
        vmem((ys * ustride, LANES), F32),
        vmem((ITERS, ys, xs, nz), F32),
        vmem((ys, xs, LANES), F32),
        vmem((ITERS, 2 * PAD, flat), F32),
        vmem((ITERS, 2 * PAD, flat), F32),
        vmem((ITERS, 2 * PAD, flat), F32),
        vmem((ITERS, 2 * PAD, flat), F32),
        vmem((ITERS, 2, PAD, xs, nz), F32),
        vmem((ITERS, sides, ny, PAD, nz), F32),
        vmem((ITERS, 2, PAD, xs, nz), F32),
        vmem((ITERS, sides, ny, PAD, nz), F32),
        vmem((STATS, views, 8, nz), F32),
        vmem((ITERS, 3, peak, STATS * 8, LANES), F32),
        vmem((ITERS, 3, STATS * 8, LANES), F32),
        vmem((vx, LANES), F32),
        vmem((vx, 2 * xs), F32),
        vmem((xs, 2 * vx), BF16),
        vmem((views, ny, 2 * ys), BF16),
        vmem((views, ys, 2 * ny), BF16),
        vmem((views, 2 * nz, nz), BF16),
        vmem((views, 2 * LANES, nz), BF16),
        vmem((views, 2 * nz, nz + LANES), BF16),
        pltpu.SemaphoreType.DMA(()),
        pltpu.SemaphoreType.DMA((ITERS, 12)),
        pltpu.SemaphoreType.DMA((ITERS, 12)),
        pltpu.SemaphoreType.DMA((ITERS, 3, peak)),
        pltpu.SemaphoreType.DMA((ITERS, 3, peak)),
    ]
    smem = pl.BlockSpec(memory_space=pltpu.SMEM)
    inside = pl.BlockSpec(memory_space=pltpu.VMEM)
    out, misfit = pl.pallas_call(
        functools.partial(kernel, (counts, (views, nx, ny, nz))),
        out_shape=[
            jax.ShapeDtypeStruct((nx * ny, nz), F32),
            jax.ShapeDtypeStruct((ITERS, views), F32),
        ],
        in_specs=[smem, smem, inside, pl.BlockSpec(memory_space=pl.ANY)],
        out_specs=[inside, inside],
        scratch_shapes=scratch,
        compiler_params=pltpu.CompilerParams(
            collective_id=0, has_side_effects=True, vmem_limit_bytes=60 * 1024 * 1024
        ),
    )(psf_taps, view_weights, estimate.reshape(nx * ny, nz), view_images.reshape(views * nx * ny, nz))
    return out.reshape(nx, ny, nz), misfit


def solution(mesh):
    counts = tuple(mesh.shape[a] for a in AXES)
    placed = (P("gx", "gy", "gz"), P(None, "gx", "gy", "gz"), P(), P())
    return jax.shard_map(
        functools.partial(local, counts), mesh=mesh, in_specs=placed,
        out_specs=(P("gx", "gy", "gz"), P()), check_vma=False,
    )
```

time: 392 us -> 125 us (0.32); the launches traced: 386 us -> 125 us
  waiting for transfers between devices: 130 us -> 0 us
  Pallas kernels: 0 us -> 120 us
  blocking collectives: 73.7 us -> 0 us
  starting transfers between devices: 65.6 us -> 0 us
  local copies, waits for them, and re-layouts: 55.7 us -> 4.25 us
  matrix products: 48.9 us -> 0 us
  other arithmetic: 10.7 us -> 0 us
    ppermute x24 -> x0, waiting for transfers between devices: 130 us -> none  [the longest x12 77.7 us: extended(): lax.ppermute(lax.slice_in_dim(block, block.shape[dim] - width, None, axis...]
    pallas_call x0 -> x1, Pallas kernels: none -> 120 us  [local(): pl.pallas_call(functools.partial(kernel, (counts, (views, nx, ny, nz))),...]
    psum x2 -> x0, blocking collectives: 73.7 us -> none  [the longest x1 36.9 us: local(): lax.psum((local_total, jnp.sum(view_images * blurred, axis=(1, 2, 3)), jn...]
    ppermute x24 -> x0, starting transfers between devices: 65.6 us -> none  [the longest x12 45.2 us: extended(): lax.ppermute(lax.slice_in_dim(block, block.shape[dim] - width, None, axis...]
    dot_general x18 -> x0, matrix products: 48.9 us -> none  [the longest x12 45.4 us: product(): return jnp.einsum(form, left, right, precision=lax.Precision.HIGHEST)]
    slice x20 -> x0, local copies, waits for them, and re-layouts: 32.2 us -> none  [the longest x16 23.2 us: extended(): lax.slice_in_dim(block, block.shape[dim] - width, None, axis=dim)]
    ppermute x8 -> x0, local copies, waits for them, and re-layouts: 22.1 us -> none  [the longest x4 11.6 us: extended(): lax.ppermute(lax.slice_in_dim(block, 0, width, axis=dim), axis, backward)]
    concatenate x7 -> x0, other arithmetic: 4.44 us -> none  [extended(): block = jnp.concatenate([low, block, high], axis=dim)]
  transfers between devices with their start and end apart: 24 -> 0, of which waited for: 24 -> 0; matrix products, arithmetic and copies ran while one was open for 6% -> 0% of each run, Pallas kernels for 0% -> 0%
where the time goes in v1:
time: 125 us
  Pallas kernels  120 us (96%)
  local copies, waits for them, and re-layouts  4.25 us (3%)
    pallas_call x1, Pallas kernels, local(): pl.pallas_call(functools.partial(kernel, (counts, (views, nx, ny, nz))),...  120 us
    unnamed x3, local copies, waits for them, and re-layouts  4.25 us

profile of v1, /device:TPU:1, one launch (start us, length us, event | category | flops | bytes accessed | tf_op | source)
XLA Modules:
  0.0 124.8 jit_solution(12808925892109171349)
XLA Ops:
  0.6 1.3 %copy.6.taps_ref = s32[4,3,31]{2,1,0:T(4,128)} copy(s32[4,3,31]{2,0,1:T(4,128)} %param.6) | data formatting | bytes 2976 | tf_op args[2]
  1.9 119.9 %shard_map.59 = (f32[768,128]{1,0:T(8,128)}, f32[2,4]{1,0:T(2,128)}) custom-call(s32[4,3,31]{2,1,0:T(4,128)} %copy.6.taps_ref, s32[4]{0:T(128)} %weights_ref.1, f32[768,128]{1,0:T(8,128)} %bitcast.5, f32[3072,128]{1,0:T(8,128)} %bitcast.3), custom_call_target="tpu_custom_call" | custom-call | tf_op jit(solution)/shard_map/pallas_call | solution.py:475
  121.9 1.8 %copy.9 = f32[24,32,128]{2,1,0:T(8,128)} copy(f32[24,32,128]{2,1,0:T(8,128)} %bitcast.4) | data formatting | bytes 786432
  123.6 1.2 copy.10

commit v2 on v1

v2 whole, which is shorter than its diff:
```python
import functools

import jax
import jax.numpy as jnp
from jax import lax
from jax.experimental import pallas as pl
from jax.experimental.pallas import tpu as pltpu
from jax.sharding import PartitionSpec as P

TAPS = 31
ITERS = 2
REACH = 15
PAD = 16
LANES = 128
MESH = pl.DeviceIdType.MESH
AXES = ("gx", "gy", "gz")
F32 = jnp.float32
BF16 = jnp.bfloat16
STATS = 5


def halves(value, axis):
    high = value.astype(BF16).astype(F32)
    return jnp.concatenate([high, value - high], axis=axis).astype(BF16)


def dot(left, right):
    return jnp.dot(left, right, preferred_element_type=F32)


def dot_nt(left, right):
    return lax.dot_general(left, right, (((1,), (1,)), ((), ())), preferred_element_type=F32)


def dot_tn(left, right):
    return lax.dot_general(left, right, (((0,), (0,)), ((), ())), preferred_element_type=F32)


def iota(shape, dim):
    return lax.broadcasted_iota(jnp.int32, shape, dim)


class Shift:
    def __init__(self, axis, count, step, source, target, send_sem, recv_sem, swap=False):
        me = lax.axis_index(axis)
        if swap:
            self.sends = self.receives = None
            goal = 1 - me
        else:
            self.sends = (me + step >= 0) & (me + step < count)
            self.receives = (me - step >= 0) & (me - step < count)
            goal = me + step
        self.copy = pltpu.make_async_remote_copy(
            src_ref=source, dst_ref=target, send_sem=send_sem, recv_sem=recv_sem,
            device_id={axis: goal}, device_id_type=MESH,
        )

    def when(self, condition, action):
        if condition is None:
            action()
        else:
            pl.when(condition)(action)

    def start(self):
        self.when(self.sends, self.copy.start)

    def wait_recv(self):
        self.when(self.receives, self.copy.wait_recv)

    def wait_send(self):
        self.when(self.sends, self.copy.wait_send)


def kernel(sizes, taps_ref, weights_ref, est_ref, images_ref, out_ref, misfit_ref,
           img, eo, xr, ya, yb, eho, ehx, eha, ehy, t1, t2, t3, t4, fo, fh, quo, uo, uh,
           ca, cb, cha, chb, ba, bb, ra, rb, rx, stats, ar1, ar2, ar_own, scale,
           kx, kxb, ky, kyb, kz, kzh, kzb, img_sem, send, recv, ar_send, ar_recv):
    counts, (views, nx, ny, nz) = sizes
    swap = counts[0] == 2
    sides = 1 if swap else 2
    xs = nx + sides * PAD
    ys = ny + 2 * PAD
    fstride = fo.shape[0] // (views * nx)
    ustride = uo.shape[0] // ys
    chunk = 8
    rows = chunk * ny
    blocks = nx // chunk
    mx, my, mz = (lax.axis_index(a) for a in AXES)

    image_copy = pltpu.make_async_copy(images_ref, img, img_sem)
    image_copy.start()

    plane = [(p, q) for p in range(counts[0]) for q in range(counts[1]) if p or q]
    barrier = pltpu.get_barrier_semaphore()

    def in_plane(p, q):
        return {"gx": lax.rem(mx + p, counts[0]), "gy": lax.rem(my + q, counts[1])}

    for p, q in plane:
        pl.semaphore_signal(barrier, inc=1, device_id=in_plane(p, q), device_id_type=MESH)
    for p in range(1, counts[2]):
        pl.semaphore_signal(barrier, inc=1, device_id={"gz": lax.rem(mz + p, counts[2])}, device_id_type=MESH)

    for y in range(ny):
        eo[0, y] = est_ref[pl.ds(y, nx, stride=ny), :]

    pl.semaphore_wait(barrier, len(plane) + counts[2] - 1)

    face = pl.multiple_of((1 - mx) * (nx - PAD), 8) if swap else None
    low, high = pl.ds(0, PAD), pl.ds(PAD, PAD)
    tail = pl.ds(ny - PAD, PAD)
    used = [0] * ITERS

    def shift(it, axis, step, source, target, swap=False):
        k = used[it]
        used[it] += 1
        return Shift(axis, counts[AXES.index(axis)], step, source, target, send.at[it, k], recv.at[it, k], swap)

    def start(copies):
        for c in copies:
            c.start()
        return copies

    def arrive(copies):
        for c in copies:
            c.wait_recv()
            c.wait_send()

    def x_gather(it):
        if swap:
            return start([shift(it, "gx", 1, eo.at[it, :, pl.ds(face, PAD), :], xr.at[it, 0], swap=True)])
        return start([
            shift(it, "gx", 1, eo.at[it, :, pl.ds(nx - PAD, PAD), :], xr.at[it, 0]),
            shift(it, "gx", -1, eo.at[it, :, low, :], xr.at[it, 1]),
        ])

    def y_gather(it, source, target):
        return start([
            shift(it, "gy", 1, source.at[tail], target(0)),
            shift(it, "gy", -1, source.at[low], target(1)),
        ])

    def z_pair(it, buffer):
        return start([
            shift(it, "gz", 1, buffer.at[it, 0, high], buffer.at[it, 1, low]),
            shift(it, "gz", -1, buffer.at[it, 0, low], buffer.at[it, 1, high]),
        ])

    def y_reduce(it, source, target):
        return start([
            shift(it, "gy", 1, source.at[pl.ds(PAD + ny, PAD)], target.at[0]),
            shift(it, "gy", -1, source.at[low], target.at[1]),
        ])

    def x_reduce(it):
        own = pl.ds(PAD, ny)
        if swap:
            return start([shift(it, "gx", 1, cb.at[it, 0, own], rx.at[it, 0], swap=True)])
        return start([
            shift(it, "gx", 1, cb.at[it, 1, own], rx.at[it, 0]),
            shift(it, "gx", -1, cb.at[it, 0, own], rx.at[it, 1]),
        ])

    def edges():
        def clear(condition, refs):
            @pl.when(condition)
            def _():
                for ref in refs:
                    ref[...] = jnp.zeros(ref.shape, F32)
        both = range(ITERS)
        for d, edge in ((0, my == 0), (1, my == counts[1] - 1)):
            clear(edge, [r for it in both for r in (ya.at[it, d], yb.at[it, d], ra.at[it, d])]
                  + [rb.at[it, s, d] for it in both for s in range(sides)])
        for part, edge in ((low, mz == 0), (high, mz == counts[2] - 1)):
            clear(edge, [r.at[it, 1, part] for it in both for r in (t1, t2, t3, t4, ba, bb)])
        if not swap:
            for d, edge in ((0, mx == 0), (1, mx == counts[0] - 1)):
                clear(edge, [r.at[it, d] for it in both for r in (xr, rx)])

    def x_position(slot):
        if swap:
            return jnp.where(slot < nx, slot, slot - jnp.where(mx == 0, 0, nx + PAD))
        return jnp.where(slot < nx, slot, jnp.where(slot < nx + PAD, slot - nx - PAD, slot - PAD))

    def z_position(slot):
        position = jnp.where(slot < PAD, slot - PAD, slot - PAD + nz)
        return jnp.where(slot < 2 * PAD, position, -nz * 4)

    def fill(view, dim, offsets):
        def step(t, total):
            tap = taps_ref[view, dim, t].astype(F32) * (1.0 / 256.0)
            return tuple(jnp.where(o == t, tap, m) for o, m in zip(offsets, total))
        return lax.fori_loop(0, TAPS, step, tuple(jnp.zeros(o.shape, F32) for o in offsets), unroll=4)

    def pair(value, axis):
        return jnp.concatenate([value, value], axis=axis).astype(BF16)

    def matrices():
        columns = []
        for v in range(views):
            f_shape, b_shape = (nx, xs), (xs, nx)
            f, b = fill(v, 0, (
                x_position(iota(f_shape, 1)) - iota(f_shape, 0) + REACH,
                x_position(iota(b_shape, 0)) - iota(b_shape, 1) + REACH,
            ))
            kx[pl.ds(v * nx, nx), 0:xs] = f
            kx[pl.ds(v * nx, nx), xs:2 * xs] = f
            columns.append(b)
            f_shape, b_shape = (ny, ys), (ys, ny)
            f, b = fill(v, 1, (
                iota(f_shape, 1) - PAD - iota(f_shape, 0) + REACH,
                iota(b_shape, 0) - PAD - iota(b_shape, 1) + REACH,
            ))
            ky[v] = pair(f, 1)
            kyb[v] = pair(b, 1)
            square = (nz, nz)
            halo = (LANES, nz)
            back = (nz, LANES)
            f, h = fill(v, 2, (
                iota(square, 0) - iota(square, 1) + REACH,
                z_position(iota(halo, 0)) - iota(halo, 1) + REACH,
            ))
            kz[v] = pair(f, 0)
            kzh[v] = pair(h, 0)
            f, b = fill(v, 2, (
                iota(square, 1) - iota(square, 0) + REACH,
                z_position(iota(back, 1)) - iota(back, 0) + REACH,
            ))
            kzb[v, :, 0:nz] = pair(f, 0)
            kzb[v, :, nz:nz + LANES] = pair(b, 0)
        kxb[...] = jnp.concatenate(columns + columns, axis=1).astype(BF16)


    picks = (2 * PAD, LANES)
    ends = jnp.where(iota(picks, 0) < PAD, iota(picks, 0), iota(picks, 0) + nz - 2 * PAD)
    pick_ends = (iota(picks, 1) == ends).astype(F32)
    pick_first = (iota(picks, 1) == iota(picks, 0)).astype(F32)
    ends_wide, first_wide = pair(pick_ends, 1), pair(pick_first, 1)
    ends_tall, first_tall = pair(pick_ends, 0), pair(pick_first, 0)

    normalizer = jnp.float32(0.0)
    for v in range(views):
        product = jnp.float32(1.0)
        for d in range(3):
            total = lax.fori_loop(0, TAPS, lambda t, s, v=v, d=d: s + taps_ref[v, d, t], jnp.int32(0))
            product = product * (total.astype(F32) * (1.0 / 256.0))
        normalizer = normalizer + weights_ref[v].astype(F32) * product

    def loop(count, body, unroll=8):
        unroll = max(u for u in range(1, unroll + 1) if count % u == 0)
        def step(i, carry):
            for u in range(unroll):
                body(i * unroll + u)
            return carry
        if unroll == count:
            step(0, 0)
        else:
            lax.fori_loop(0, count // unroll, step, 0)

    def blur_x(sources, target, count, first):
        matrix = kx[...].astype(BF16)
        def body(y):
            block = jnp.concatenate([r[y] for r in sources], axis=0)
            target[pl.ds(first + y, views * nx, stride=fstride), :] = dot(matrix, halves(block, 0))
        loop(count, body)

    def blur_own(own, beside, target):
        blur_x([own] + [beside.at[s] for s in range(sides)], target, ny, PAD)

    def blur_halo(own, beside, target):
        for d in range(2):
            blur_x([own.at[d]] + [beside.at[d, s] for s in range(sides)], target, PAD, d * (PAD + ny))

    def spread_x(source, target_own, target_side):
        matrix = kxb[...]
        weight = scale[...]
        def body(y):
            value = source[pl.ds(pl.multiple_of(y * ustride, 8), views * nx), :] * weight
            value = dot(matrix, halves(value, 0))
            target_own[y] = value[0:nx]
            for s in range(sides):
                target_side[s, y] = value[nx + s * PAD:nx + (s + 1) * PAD]
        loop(ys, body)

    def flat(ref):
        count = 1
        for d in ref.shape[:-1]:
            count *= d
        return ref.reshape(count, LANES), count // LANES

    def turned(it, source, buffer, select):
        ref, pieces = flat(source)
        def body(i):
            at = pl.ds(pl.multiple_of(i * LANES, LANES), LANES)
            buffer[it, 0, :, at] = dot_nt(select, halves(ref[at, :], 1))
        loop(pieces, body)

    def unturned(it, buffer, select, target, add):
        ref, pieces = flat(target)
        def body(i):
            at = pl.ds(pl.multiple_of(i * LANES, LANES), LANES)
            value = dot_tn(halves(buffer[it, 1, :, at], 0), select)
            ref[at, :] = ref[at, :] + value if add else value
        loop(pieces, body)

    for it in range(ITERS):
        last = it == ITERS - 1
        if it == 0:
            sent_x = x_gather(0)
        sent_y = y_gather(it, eo.at[it], lambda d: ya.at[it, d])
        turned(it, eo.at[it], t1, ends_wide)
        sent_1 = z_pair(it, t1)
        if it == 0:
            edges()
            matrices()
        arrive(sent_y)
        turned(it, ya.at[it], t2, ends_wide)
        sent_2 = z_pair(it, t2)
        arrive(sent_1)
        unturned(it, t1, first_tall, eho, False)
        arrive(sent_x)
        sent_y = []
        for s in range(sides):
            sent_y += y_gather(it, xr.at[it, s], lambda d, s=s: yb.at[it, d, s])
        turned(it, xr.at[it], t3, ends_wide)
        sent_3 = z_pair(it, t3)
        arrive(sent_2)
        unturned(it, t2, first_tall, eha, False)
        blur_own(eo.at[it], xr.at[it], fo)
        arrive(sent_y)
        turned(it, yb.at[it], t4, ends_wide)
        sent_4 = z_pair(it, t4)
        blur_halo(ya.at[it], yb.at[it], fo)
        arrive(sent_3)
        unturned(it, t3, first_tall, ehx, False)
        blur_own(eho, ehx, fh)
        arrive(sent_4)
        unturned(it, t4, first_tall, ehy, False)
        blur_halo(eha, ehy, fh)

        if it == 0:
            image_copy.wait()
        stats[...] = jnp.zeros_like(stats)

        def forward(i, carry):
            v = i // blocks
            base = i * chunk
            own, side = [], []
            for u in range(chunk):
                at = pl.ds(pl.multiple_of((base + u) * fstride, 8), ys)
                both = jnp.concatenate([fo[at, :], fh[at, :]], axis=1)
                value = dot(ky[v], halves(both, 0))
                own.append(value[:, 0:nz])
                side.append(value[:, nz:nz + LANES])
            blurred = dot(halves(jnp.concatenate(own, axis=0), 1), kz[v])
            blurred = blurred + dot(halves(jnp.concatenate(side, axis=0), 1), kzh[v])
            at = pl.ds(pl.multiple_of(i * rows, rows), rows)
            image = img[at, :]
            quo[at, :] = image / blurred
            terms = [blurred, image * blurred, blurred * blurred, image, image * image]
            for k, term in enumerate(terms):
                folded = jnp.sum(term.reshape(rows // 8, 8, nz), axis=0)
                stats[k, v] = stats[k, v] + folded
            return carry

        lax.fori_loop(0, views * blocks, forward, 0, unroll=2)

        def reduce_start(k, value, buffer, peers):
            ar_own[it, k] = value
            copies = []
            for n, peer in enumerate(peers):
                c = pltpu.make_async_remote_copy(
                    src_ref=ar_own.at[it, k], dst_ref=buffer.at[it, n],
                    send_sem=ar_send.at[it, k, n], recv_sem=ar_recv.at[it, k, n],
                    device_id=peer, device_id_type=MESH,
                )
                c.start()
                copies.append(c)
            return copies

        def tree(terms):
            while len(terms) > 1:
                half = len(terms) // 2
                terms = [terms[i] + terms[i + half] for i in range(half)] + terms[2 * half:]
            return terms[0]

        def backward(low, high):
            def step(i, carry):
                v = i // blocks
                at = pl.ds(pl.multiple_of(i * rows, rows), rows)
                wide = dot(halves(quo[at, :], 1), kzb[v])
                for u in range(chunk):
                    value = dot(kyb[v], halves(wide[u * ny:(u + 1) * ny], 0))
                    at = pl.ds(i * chunk + u, ys, stride=ustride)
                    uo[at, :] = value[:, 0:nz]
                    uh[at, :] = value[:, nz:nz + LANES]
                return carry
            lax.fori_loop(low, high, step, 0, unroll=2)

        lane = iota((8, LANES), 1)
        block = jnp.zeros((8, LANES), F32)
        for k in range(STATS):
            sums = jnp.concatenate(
                [jnp.sum(stats[k, v], axis=0, keepdims=True) for v in range(views)]
                + [jnp.ones((8 - views, LANES), F32)], axis=0)
            block = jnp.where(lane == k, jnp.sum(sums, axis=1, keepdims=True), block)
        steps = views * blocks
        copies = reduce_start(0, block, ar1, [in_plane(p, q) for p, q in plane])
        backward(0, steps // 2)
        for c in copies:
            c.wait()
        terms = {pq: ar1[it, n] for n, pq in enumerate(plane)}
        terms[0, 0] = ar_own[it, 0]
        block = tree([tree([terms[p, q] for p in range(counts[0])]) for q in range(counts[1])])
        copies = reduce_start(1, block, ar2, [{"gz": lax.rem(mz + p, counts[2])} for p in range(1, counts[2])])
        backward(steps // 2, steps)
        for c in copies:
            c.wait()
        block = tree([ar_own[it, 1]] + [ar2[it, n] for n in range(counts[2] - 1)])
        blurred_total, cross, square, data_total, data_square = (
            jnp.broadcast_to(block[:, k:k + 1], block.shape) for k in range(STATS))
        flux = data_total / blurred_total
        misfit = (data_square - 2.0 * flux * cross + flux * flux * square) / data_square
        line = jnp.sum(jnp.where(lane == iota(misfit.shape, 0), misfit, 0.0), axis=0, keepdims=True)
        misfit_ref[it:it + 1, :] = line[:, 0:views]
        for v in range(views):
            top = jnp.full((1, LANES), weights_ref[v].astype(F32), F32)
            row = top / (jnp.full((1, LANES), normalizer, F32) * flux[v:v + 1])
            scale[pl.ds(v * nx, nx), :] = jnp.broadcast_to(row, (nx, LANES))

        spread_x(uh, cha, chb)
        turned(it, chb, bb, first_wide)
        sent_b = z_pair(it, bb)
        turned(it, cha, ba, first_wide)
        sent_a = z_pair(it, ba)
        spread_x(uo, ca.at[it], cb.at[it])
        arrive(sent_b)
        unturned(it, bb, ends_tall, cb.at[it], True)
        sent_b = []
        for s in range(sides):
            sent_b += y_reduce(it, cb.at[it, s], rb.at[it, s])
        arrive(sent_a)
        unturned(it, ba, ends_tall, ca.at[it], True)
        sent_a = y_reduce(it, ca.at[it], ra.at[it])
        arrive(sent_b)
        for s in range(sides):
            for y in range(PAD):
                cb[it, s, PAD + y] = cb[it, s, PAD + y] + rb[it, s, 0, y]
                cb[it, s, ny + y] = cb[it, s, ny + y] + rb[it, s, 1, y]
        sent_x = x_reduce(it)
        arrive(sent_a)
        for y in range(PAD):
            ca[it, PAD + y] = ca[it, PAD + y] + ra[it, 0, y]
            ca[it, ny + y] = ca[it, ny + y] + ra[it, 1, y]
        arrive(sent_x)
        for y in range(ny):
            if swap:
                at = pl.ds(face, PAD)
                ca[it, PAD + y, at, :] = ca[it, PAD + y, at, :] + rx[it, 0, y]
            else:
                ca[it, PAD + y, low, :] = ca[it, PAD + y, low, :] + rx[it, 0, y]
                at = pl.ds(nx - PAD, PAD)
                ca[it, PAD + y, at, :] = ca[it, PAD + y, at, :] + rx[it, 1, y]
            value = eo[it, y] * ca[it, PAD + y]
            if last:
                out_ref[pl.ds(y, nx, stride=ny), :] = value
            else:
                eo[it + 1, y] = value
        if not last:
            sent_x = x_gather(it + 1)


def local(counts, estimate, view_images, psf_taps, view_weights):
    views, nx, ny, nz = view_images.shape
    sides = 1 if counts[0] == 2 else 2
    xs = nx + sides * PAD
    ys = ny + 2 * PAD
    vx = views * nx
    peak = max(counts[0] * counts[1], counts[2])
    fstride, ustride = ys + 8, vx + 8
    vmem = pltpu.VMEM
    own_own, own_halo, halo_own, halo_halo = ny * nx, 2 * PAD * nx, sides * ny * PAD, 2 * sides * PAD * PAD
    scratch = [
        vmem((views * nx * ny, nz), F32),
        vmem((ITERS, ny, nx, nz), F32),
        vmem((ITERS, sides, ny, PAD, nz), F32),
        vmem((ITERS, 2, PAD, nx, nz), F32),
        vmem((ITERS, 2, sides, PAD, PAD, nz), F32),
        vmem((ny, nx, LANES), F32),
        vmem((sides, ny, PAD, LANES), F32),
        vmem((2, PAD, nx, LANES), F32),
        vmem((2, sides, PAD, PAD, LANES), F32),
        vmem((ITERS, 2, 2 * PAD, own_own), F32),
        vmem((ITERS, 2, 2 * PAD, own_halo), F32),
        vmem((ITERS, 2, 2 * PAD, halo_own), F32),
        vmem((ITERS, 2, 2 * PAD, halo_halo), F32),
        vmem((vx * fstride, nz), F32),
        vmem((vx * fstride, LANES), F32),
        vmem((views * nx * ny, nz), F32),
        vmem((ys * ustride, nz), F32),
        vmem((ys * ustride, LANES), F32),
        vmem((ITERS, ys, nx, nz), F32),
        vmem((ITERS, sides, ys, PAD, nz), F32),
        vmem((ys, nx, LANES), F32),
        vmem((sides, ys, PAD, LANES), F32),
        vmem((ITERS, 2, 2 * PAD, ys * nx), F32),
        vmem((ITERS, 2, 2 * PAD, sides * ys * PAD), F32),
        vmem((ITERS, 2, PAD, nx, nz), F32),
        vmem((ITERS, sides, 2, PAD, PAD, nz), F32),
        vmem((ITERS, sides, ny, PAD, nz), F32),
        vmem((STATS, views, 8, nz), F32),
        vmem((ITERS, counts[0] * counts[1], 8, LANES), F32),
        vmem((ITERS, counts[2], 8, LANES), F32),
        vmem((ITERS, 2, 8, LANES), F32),
        vmem((vx, LANES), F32),
        vmem((vx, 2 * xs), F32),
        vmem((xs, 2 * vx), BF16),
        vmem((views, ny, 2 * ys), BF16),
        vmem((views, ys, 2 * ny), BF16),
        vmem((views, 2 * nz, nz), BF16),
        vmem((views, 2 * LANES, nz), BF16),
        vmem((views, 2 * nz, nz + LANES), BF16),
        pltpu.SemaphoreType.DMA(()),
        pltpu.SemaphoreType.DMA((ITERS, 32)),
        pltpu.SemaphoreType.DMA((ITERS, 32)),
        pltpu.SemaphoreType.DMA((ITERS, 2, peak)),
        pltpu.SemaphoreType.DMA((ITERS, 2, peak)),
    ]
    smem = pl.BlockSpec(memory_space=pltpu.SMEM)
    inside = pl.BlockSpec(memory_space=pltpu.VMEM)
    out, misfit = pl.pallas_call(
        functools.partial(kernel, (counts, (views, nx, ny, nz))),
        out_shape=[
            jax.ShapeDtypeStruct((nx * ny, nz), F32),
            jax.ShapeDtypeStruct((ITERS, views), F32),
        ],
        in_specs=[smem, smem, inside, pl.BlockSpec(memory_space=pl.ANY)],
        out_specs=[inside, inside],
        scratch_shapes=scratch,
        compiler_params=pltpu.CompilerParams(
            collective_id=0, has_side_effects=True, vmem_limit_bytes=60 * 1024 * 1024
        ),
    )(psf_taps, view_weights, estimate.reshape(nx * ny, nz), view_images.reshape(views * nx * ny, nz))
    return out.reshape(nx, ny, nz), misfit


def solution(mesh):
    counts = tuple(mesh.shape[a] for a in AXES)
    placed = (P("gx", "gy", "gz"), P(None, "gx", "gy", "gz"), P(), P())
    return jax.shard_map(
        functools.partial(local, counts), mesh=mesh, in_specs=placed,
        out_specs=(P("gx", "gy", "gz"), P()), check_vma=False,
    )
```

time: 125 us -> 96 us (0.77)
  Pallas kernels: 120 us -> 90.8 us
    pallas_call x1, Pallas kernels: 120 us -> 90.8 us  [local(): pl.pallas_call(functools.partial(kernel, (counts, (views, nx, ny, nz))),...]
where the time goes in v2:
time: 96 us; the launch traced here: 95.7 us
  Pallas kernels  90.8 us (95%)
  local copies, waits for them, and re-layouts  4.25 us (4%)
    pallas_call x1, Pallas kernels, local(): pl.pallas_call(functools.partial(kernel, (counts, (views, nx, ny, nz))),...  90.8 us
    unnamed x3, local copies, waits for them, and re-layouts  4.25 us

profile of v2, /device:TPU:1, one launch (start us, length us, event | category | flops | bytes accessed | tf_op | source)
XLA Modules:
  0.0 95.7 jit_solution(17422786911684635636)
XLA Ops:
  0.6 1.3 %copy.6.taps_ref = s32[4,3,31]{2,1,0:T(4,128)} copy(s32[4,3,31]{2,0,1:T(4,128)} %param.6) | data formatting | bytes 2976 | tf_op args[2]
  1.9 90.8 %shard_map.59 = (f32[768,128]{1,0:T(8,128)}, f32[2,4]{1,0:T(2,128)}) custom-call(s32[4,3,31]{2,1,0:T(4,128)} %copy.6.taps_ref, s32[4]{0:T(128)} %weights_ref.1, f32[768,128]{1,0:T(8,128)} %bitcast.5, f32[3072,128]{1,0:T(8,128)} %bitcast.3), custom_call_target="tpu_custom_call" | custom-call | tf_op jit(solution)/shard_map/pallas_call | solution.py:531
  92.7 1.8 %copy.9 = f32[24,32,128]{2,1,0:T(8,128)} copy(f32[24,32,128]{2,1,0:T(8,128)} %bitcast.4) | data formatting | bytes 786432
  94.5 1.2 %copy.10 = f32[2,4]{1,0:T(2,128)} copy(f32[2,4]{1,0:T(2,128)} %get-tuple-element.9) | data formatting | bytes 64
